TPU v7x, 32 devices: a whole 2x2x4 slice. The times are simulated.
32 devices in a mesh: row: 8 (over y, x, core), col: 4 (over z).
Axes of the slice: x: 2, y: 2, z: 4, core: 2. Of those that a mesh axis runs over, the one named last changes fastest.
Arguments:
- state: float32 [2048, 4, 1024], P('row', 'col'), may hold values from -6 to 6
- coupling: bfloat16 [2048, 4, 1024], P('row', 'col'), may hold values from -2 to 2, as said below
- coupling_t: bfloat16 [2, 2048, 4, 1024], P(None, 'row', 'col'), may hold values from -2 to 2, as said below
- factor: float32 [4, 4, 256, 256], P(None, 'col', 'row'), may hold values from -0.3 to 1.3
- cofactor: float32 [4, 4, 256, 256], P(None, 'col', 'row'), may hold values from -0.3 to 1.3
- rates: float32 [4, 4, 256], P(None, 'col'), may hold values from 0.5 to 2
Outputs:
- updated_state: float32 [2048, 4, 1024], P('row', 'col')
Inputs may be any that keep to these rules, and one draw needn't show every extreme that they name: coupling and coupling_t hold the same matrix A; its blocks A(i, k) are zero unless k > i. coupling_t holds the transposed blocks of the A in coupling.
All inputs are finite; a program needn't handle non-finite values.
Results may differ from a plain program's by a relative error of at most 0.0003.
Values may be sent and summed in bfloat16 or wider, within the bound.
A program may use at most 64 MiB of HBM per device.

v0:
```python
import jax
import jax.numpy as jnp
from jax import lax
from jax.sharding import PartitionSpec as P

STEPS = 2
HIGHEST_PRECISION = lax.Precision.HIGHEST


def broadcast(block, axis, source):
    block = jnp.where(lax.axis_index(axis) == source, block, jnp.zeros_like(block))
    return lax.psum(block, axis)


def from_behind(block, axis, distance):
    devices = range(lax.axis_size(axis))
    route = [((i - distance) % len(devices), i) for i in devices]
    return lax.ppermute(block, axis, route)


def solve_block(residual, left_p, left_q, left_e, right_p, right_q, right_e):
    middle = jnp.dot(
        left_q, residual, precision=HIGHEST_PRECISION, preferred_element_type=jnp.float32
    )
    middle = jnp.dot(
        middle, right_q.T, precision=HIGHEST_PRECISION, preferred_element_type=jnp.float32
    )
    middle = middle / (left_e[:, None] + right_e[None, :])
    product = jnp.dot(
        left_p, middle, precision=HIGHEST_PRECISION, preferred_element_type=jnp.float32
    )
    return -jnp.dot(
        product, right_p.T, precision=HIGHEST_PRECISION, preferred_element_type=jnp.float32
    )


def pick_slot(stacked, slot_index):
    return lax.dynamic_index_in_dim(stacked, slot_index, 0, keepdims=False)


def on_device(state, coupling, coupling_t, factor, cofactor, rates):
    row_count = lax.axis_size("row")
    col_count = lax.axis_size("col")
    half_rows = row_count // 2
    order_blocks = 2 * row_count
    col_slots = order_blocks // col_count
    block_size = state.shape[0]
    row_index = lax.axis_index("row")
    col_index = lax.axis_index("col")
    blocks = jnp.transpose(state.reshape(block_size, col_slots, block_size), (1, 0, 2))
    full_p, full_q = (
        lax.all_gather(factor, "row", axis=2, tiled=True),
        lax.all_gather(cofactor, "row", axis=2, tiled=True),
    )
    right_ps = full_p.reshape(col_slots, block_size, block_size)
    right_qs = full_q.reshape(col_slots, block_size, block_size)
    right_es = rates.reshape(col_slots, block_size)
    own_slot = row_index // col_count
    picked = (
        pick_slot(right_ps, own_slot),
        pick_slot(right_qs, own_slot),
        pick_slot(right_es, own_slot),
    )
    left_p, left_q, left_e = (
        broadcast(picked[0], "col", row_index % col_count),
        broadcast(picked[1], "col", row_index % col_count),
        broadcast(picked[2], "col", row_index % col_count),
    )
    upper_row = coupling.reshape(block_size, col_slots * block_size)
    lower_pair = coupling_t.reshape(2, block_size, col_slots * block_size)
    my_columns = col_index + col_count * jnp.arange(col_slots, dtype=jnp.int32)
    upper_now = upper_row
    for wave_step in range(STEPS):
        antidiag = order_blocks - 1 - wave_step
        partner = antidiag - row_index
        owner_col = partner % col_count
        slot_here = partner // col_count
        usable = row_index <= partner
        residual = pick_slot(blocks, slot_here)
        solution = solve_block(
            residual,
            left_p,
            left_q,
            left_e,
            pick_slot(right_ps, slot_here),
            pick_slot(right_qs, slot_here),
            pick_slot(right_es, slot_here),
        )
        solution = jnp.where(usable, solution, 0.0)
        written = jnp.where(usable & (col_index == owner_col), solution, residual)
        blocks = lax.dynamic_update_index_in_dim(blocks, written, slot_here, 0)
        shared = broadcast(solution, "col", owner_col)
        mirror = antidiag - my_columns
        use_row = mirror <= my_columns
        sources = jnp.clip(jnp.where(use_row, mirror, my_columns), 0, row_count - 1)
        offered = jnp.where((sources == row_index)[:, None, None], shared[None], 0.0)
        fetched = lax.psum(offered, "row")
        partner_blocks = jnp.where(use_row[:, None, None], fetched, jnp.swapaxes(fetched, 1, 2))
        if wave_step > 0:
            upper_now = from_behind(upper_row, "col", (col_count - wave_step) % col_count)
        receiver = (row_index - wave_step - half_rows) % row_count
        send_slot = jnp.where(receiver + wave_step >= row_count, 1, 0)
        send_piece = pick_slot(lower_pair, send_slot)
        lower_now = from_behind(send_piece, "row", (half_rows - wave_step) % row_count)
        upper_view = upper_now.reshape(block_size, col_slots, block_size)
        rolled = jnp.where(
            (col_index + wave_step) // col_count == 1, jnp.roll(upper_view, -1, axis=1), upper_view
        )
        lower_view = lower_now.reshape(block_size, col_slots, block_size)
        left_terms = jnp.einsum(
            "aub,ubc->uac", rolled.astype(jnp.float32), partner_blocks, precision=HIGHEST_PRECISION
        )
        right_terms = jnp.einsum(
            "ab,buc->uac", shared, lower_view.astype(jnp.float32), precision=HIGHEST_PRECISION
        )
        targets = (row_index <= my_columns) & (row_index + my_columns < antidiag)
        blocks = blocks - jnp.where(targets[:, None, None], left_terms + right_terms, 0.0)
    return jnp.transpose(blocks, (1, 0, 2)).reshape(block_size, 1, col_slots * block_size)


def solution(mesh):
    return jax.shard_map(
        on_device,
        mesh=mesh,
        in_specs=(
            P("row", "col", None),
            P("row", "col", None),
            P(None, "row", "col", None),
            P(None, "col", "row", None),
            P(None, "col", "row", None),
            P(None, "col", None),
        ),
        out_specs=P("row", "col", None),
        check_vma=False,
    )
```

profile of v0, /device:TPU:0, one launch (start us, length us, event | category | flops | bytes accessed | tf_op | source)
XLA Modules:
  0.0 328.6 jit_solution(1007737203448546680)
XLA Ops:
  8.1 27.3 %all-gather.3.cloned.1.call-done = f32[4,1,256,256]{3,2,1,0:T(8,128)} async-done(((f32[4,1,32,256]{3,2,1,0:T(8,128)}), f32[4,1,256,256]{3,2,1,0:T(8,128)}) %all-gather.3.cloned.1.call-update) | async-done | bytes 1048592 | tf_op jit(solution)/shard_map/all_gather | solution.py:52
  35.4 1.7 select_bitcast_fusion.1
  37.0 23.6 %all-gather.5.cloned.1.call-done = f32[4,1,256,256]{3,2,1,0:T(8,128)} async-done(((f32[4,1,32,256]{3,2,1,0:T(8,128)}), f32[4,1,256,256]{3,2,1,0:T(8,128)}) %all-gather.5.cloned.1.call-update) | async-done | bytes 1048592 | tf_op jit(solution)/shard_map/all_gather | solution.py:53
  60.7 1.7 select_bitcast_fusion
  64.2 11.9 %psum.51 = f32[256]{0:T(256)S(1)} all-reduce(f32[256]{0:T(256)S(1)} %bitcast.106), channel_id=1, replica_groups=mesh['row'=8,'col'=4] {'col'}, use_global_device_ids=true, to_apply=%region_2.3 | all-reduce | flops 256 | bytes 2048 | tf_op jit(solution)/shard_map/psum | solution.py:12
  76.1 25.7 %all-reduce.15.cloned.1.call-done = (f32[256,256]{1,0:T(8,128)}, f32[256,256]{1,0:T(8,128)}) async-done(((f32[256,256]{1,0:T(8,128)}, f32[256,256]{1,0:T(8,128)}), (f32[256,256]{1,0:T(8,128)}, f32[256,256]{1,0:T(8,128)})) %all-reduce.15.cloned.1.call-update) | async-done | bytes 524304 | tf_op jit(solution)/shard_map/psum | solution.py:12
  101.8 1.4 fusion.24
  103.2 1.4 convolution_divide_fusion.1
  105.0 1.5 bitcast_dynamic-update-slice_fusion.1
  108.5 1.5 collective-permute-start
  110.0 32.9 %all-reduce.7.cloned.1.call-done = f32[256,256]{0,1:T(8,128)} async-done(((f32[256,256]{0,1:T(8,128)}), f32[256,256]{0,1:T(8,128)}) %all-reduce.7.cloned.1.call-update) | async-done | bytes 262160 | tf_op jit(solution)/shard_map/psum | solution.py:12
  142.9 2.1 broadcast_select_fusion.1
  147.9 54.7 %all-reduce.9.cloned.1.call-done = f32[4,256,256]{1,2,0:T(8,128)} async-done(((f32[4,256,256]{1,2,0:T(8,128)}), f32[4,256,256]{1,2,0:T(8,128)}) %all-reduce.9.cloned.1.call-update) | async-done | bytes 1048592 | tf_op jit(solution)/shard_map/psum | solution.py:97
  202.5 1.6 copy.23
  204.2 1.7 fusion.7
  208.0 1.4 convolution_divide_fusion
  209.8 1.4 bitcast_dynamic-update-slice_fusion
  212.4 3.3 collective-permute-start.1
  215.7 36.9 %all-reduce.11.cloned.1.call-done = f32[256,256]{0,1:T(8,128)} async-done(((f32[256,256]{0,1:T(8,128)}), f32[256,256]{0,1:T(8,128)}) %all-reduce.11.cloned.1.call-update) | async-done | bytes 262160 | tf_op jit(solution)/shard_map/psum | solution.py:12
  252.6 2.1 broadcast_select_fusion
  258.1 54.2 %all-reduce.13.cloned.1.call-done = f32[4,256,256]{1,2,0:T(8,128)} async-done(((f32[4,256,256]{1,2,0:T(8,128)}), f32[4,256,256]{1,2,0:T(8,128)}) %all-reduce.13.cloned.1.call-update) | async-done | bytes 1048592 | tf_op jit(solution)/shard_map/psum | solution.py:97
  312.4 2.6 copy.29
  315.0 3.2 fusion.1
  318.2 3.6 %copy.32 = f32[256,1,1024]{2,1,0:T(1,128)} copy(f32[256,1,1024]{0,2,1:T(8,128)} %bitcast.98) | data formatting | bytes 2097152 | tf_op jit(solution)/shard_map/reshape | solution.py:118
  (77 shorter events, 15.3 us)
Async XLA Ops:
  6.5 55.9 %copy-start.9 = (f32[256,1,1024]{2,1,0:T(1,128)S(1)}, f32[256,1,1024]{2,1,0:T(1,128)}, u32[]{:S(2)}) copy-start(f32[256,1,1024]{2,1,0:T(1,128)} %param.6) | copy-start | bytes 3145732
  6.5 28.8 %all-gather.3.cloned.1.call-start = ((), (), s32[]{:S(2)}) async-start(), calls=%async_computation | async-start | bytes 1179648 | tf_op jit(solution)/shard_map/all_gather | solution.py:52
  7.3 53.4 %all-gather.5.cloned.1.call-start = ((), (), s32[]{:S(2)}) async-start(), calls=%async_computation.1 | async-start | bytes 1179648 | tf_op jit(solution)/shard_map/all_gather | solution.py:53
  8.0 93.8 %all-reduce.15.cloned.1.call-start = ((), (), s32[]{:S(2)}) async-start(), calls=%async_computation.6 | async-start | bytes 1048576 | tf_op jit(solution)/shard_map/psum | solution.py:12
  62.4 80.6 %all-reduce.7.cloned.1.call-start = ((), (), s32[]{:S(2)}) async-start(), calls=%async_computation.2 | async-start | bytes 524288 | tf_op jit(solution)/shard_map/psum | solution.py:12
  103.2 1.4 copy-start.5
  105.0 2.4 copy-start.10
  106.5 2.0 copy-start.2
  107.3 95.2 %all-reduce.9.cloned.1.call-start = ((), (), s32[]{:S(2)}) async-start(), calls=%async_computation.3 | async-start | bytes 2097152 | tf_op jit(solution)/shard_map/psum | solution.py:97
  108.5 39.2 %collective-permute-start = (bf16[256,1024]{1,0:T(8,128)(2,1)}, bf16[256,1024]{1,0:T(8,128)(2,1)S(1)}, u32[]{:S(2)}, u32[]{:S(2)}) collective-permute-start(bf16[256,1024]{1,0:T(8,128)(2,1)} %get-tuple-element.8), channel_id=1, source_target_pairs={{16,0},{20,4},{24,8},{28,12},{0,16},{4,20},{8,24},{12,28},{17,1},{... | collective-permute-start | bytes 1572872 | tf_op jit(solution)/shard_map/ppermute | solution.py:18
  145.0 1.0 copy-start.12
  145.0 107.6 %all-reduce.11.cloned.1.call-start = ((), (), s32[]{:S(2)}) async-start(), calls=%async_computation.4 | async-start | bytes 524288 | tf_op jit(solution)/shard_map/psum | solution.py:12
  202.5 1.7 copy-start
  204.2 1.8 copy-start.3
  204.2 1.8 copy-start.7
  206.6 1.0 copy-start.11
  208.0 1.4 copy-start.6
  209.8 2.3 copy-start.14
  211.3 1.1 copy-start.13
  212.0 100.3 %all-reduce.13.cloned.1.call-start = ((), (), s32[]{:S(2)}) async-start(), calls=%async_computation.5 | async-start | bytes 2097152 | tf_op jit(solution)/shard_map/psum | solution.py:97
  212.1 44.1 %collective-permute-start.2 = (bf16[256,1024]{1,0:T(8,128)(2,1)S(1)}, bf16[256,1024]{1,0:T(8,128)(2,1)}, u32[]{:S(2)}, u32[]{:S(2)}) collective-permute-start(bf16[256,1024]{1,0:T(8,128)(2,1)S(1)} %copy-done.14), channel_id=1, source_target_pairs={{20,0},{24,4},{28,8},{0,12},{4,16},{8,20},{12,24},{16,28},{21,1},{... | collective-permute-start | bytes 1572872 | tf_op jit(solution)/shard_map/ppermute | solution.py:18
  212.4 42.3 %collective-permute-start.1 = (bf16[256,1024]{1,0:T(8,128)(2,1)S(1)}, bf16[256,1024]{1,0:T(8,128)(2,1)S(1)}, u32[]{:S(2)}, u32[]{:S(2)}) collective-permute-start(bf16[256,1024]{1,0:T(8,128)(2,1)S(1)} %bitcast.105), channel_id=1, source_target_pairs={{1,0},{2,1},{3,2},{0,3},{5,4},{6,5},{7,6},{4,7},{9,8},{10,9},{11,1... | collective-permute-start | bytes 1572872 | tf_op jit(solution)/shard_map/ppermute | solution.py:18
  256.2 1.3 copy-start.8
  312.4 2.6 copy-start.1
  (2 other events, 1.5 us)
Sparse Core Ops, SparseCore 0:
  9.2 26.0 all-gather.2
  37.3 23.3 all-gather.4
  63.1 38.7 all-reduce.14
  107.4 35.4 all-reduce.6
  145.9 56.5 all-reduce.8
  212.2 40.3 all-reduce.10
  255.7 56.5 all-reduce.12
where the time goes:
time: 329 us
  waiting for transfers between devices  257 us (78%)
  local copies, waits for them, and re-layouts  17.3 us (5%)
  matrix products  14.4 us (4%)
  between operations  14 us (4%)
  blocking collectives  11.9 us (4%)
  other arithmetic  9.03 us (3%)
  starting transfers between devices  5.04 us (2%)
    psum x2, waiting for transfers between devices, on_device(): fetched = lax.psum(offered, 'row')  109 us
    psum x3, waiting for transfers between devices, broadcast(): return lax.psum(block, axis)  95.5 us
    all_gather x1, waiting for transfers between devices, on_device(): lax.all_gather(factor, 'row', axis=2, tiled=True)  27.3 us
    all_gather x1, waiting for transfers between devices, on_device(): lax.all_gather(cofactor, 'row', axis=2, tiled=True)  23.6 us
    psum x1, blocking collectives, broadcast(): return lax.psum(block, axis)  11.9 us
  transfers between devices with their start and end apart: 10, of which 7 were waited for; matrix products, arithmetic and copies ran while one was open for 4% of the time, Pallas kernels for 0%

commit v1 on v0

--- a/solution.py
+++ b/solution.py
@@ -94,7 +94,9 @@
         use_row = mirror <= my_columns
         sources = jnp.clip(jnp.where(use_row, mirror, my_columns), 0, row_count - 1)
         offered = jnp.where((sources == row_index)[:, None, None], shared[None], 0.0)
-        fetched = lax.psum(offered, "row")
+        fetched = offered
+        for hop in (1, 2, 4):
+            fetched = fetched + lax.ppermute(fetched, "row", [(dev, dev ^ hop) for dev in range(8)])
         partner_blocks = jnp.where(use_row[:, None, None], fetched, jnp.swapaxes(fetched, 1, 2))
         if wave_step > 0:
             upper_now = from_behind(upper_row, "col", (col_count - wave_step) % col_count)

time: 329 us -> 341 us (1.036)
  waiting for transfers between devices: 257 us -> 262 us
  starting transfers between devices: 5.04 us -> 9.29 us
    psum x2 -> x0, waiting for transfers between devices: 109 us -> none  [on_device(): fetched = lax.psum(offered, 'row')]
    ppermute x3, waiting for transfers between devices: 0.01 us -> 60 us  [from_behind(): return lax.ppermute(block, axis, route)]
    ppermute x0 -> x6, waiting for transfers between devices: none -> 52.8 us  [on_device(): lax.ppermute(fetched, 'row', [(dev, dev ^ hop) for dev in range(8)])]
    ppermute x0 -> x6, starting transfers between devices: none -> 6.29 us  [on_device(): lax.ppermute(fetched, 'row', [(dev, dev ^ hop) for dev in range(8)])]
    psum x2 -> x0, local copies, waits for them, and re-layouts: 4.26 us -> none  [on_device(): fetched = lax.psum(offered, 'row')]
    all_gather x1, waiting for transfers between devices: 27.3 us -> 23.6 us  [on_device(): lax.all_gather(factor, 'row', axis=2, tiled=True)]
    all_gather x1, waiting for transfers between devices: 23.6 us -> 27.3 us  [on_device(): lax.all_gather(cofactor, 'row', axis=2, tiled=True)]
    add x0 -> x6, other arithmetic: none -> 3.47 us  [on_device(): fetched + lax.ppermute(fetched, 'row', [(dev, dev ^ hop) for dev in range...]
  transfers between devices with their start and end apart: 10 -> 14, of which waited for: 7 -> 12; matrix products, arithmetic and copies ran while one was open for 4% -> 4% of each run, Pallas kernels for 0% -> 0%
where the time goes in v1:
time: 341 us
  waiting for transfers between devices  262 us (77%)
  matrix products  17.2 us (5%)
  local copies, waits for them, and re-layouts  15.9 us (5%)
  between operations  13.6 us (4%)
  blocking collectives  11.9 us (3%)
  other arithmetic  10.8 us (3%)
  starting transfers between devices  9.29 us (3%)
    psum x3, waiting for transfers between devices, broadcast(): return lax.psum(block, axis)  96.8 us
    ppermute x3, waiting for transfers between devices, from_behind(): return lax.ppermute(block, axis, route)  60 us
    ppermute x6, waiting for transfers between devices, on_device(): lax.ppermute(fetched, 'row', [(dev, dev ^ hop) for dev in range(8)])  52.8 us
    all_gather x1, waiting for transfers between devices, on_device(): lax.all_gather(cofactor, 'row', axis=2, tiled=True)  27.3 us
    all_gather x1, waiting for transfers between devices, on_device(): lax.all_gather(factor, 'row', axis=2, tiled=True)  23.6 us
    psum x1, blocking collectives, broadcast(): return lax.psum(block, axis)  11.9 us
  transfers between devices with their start and end apart: 14, of which 12 were waited for; matrix products, arithmetic and copies ran while one was open for 4% of the time, Pallas kernels for 0%

profile of v1, /device:TPU:0, one launch (start us, length us, event | category | flops | bytes accessed | tf_op | source)
XLA Modules:
  0.0 340.7 jit_solution(6340757194967901209)
XLA Ops:
  8.1 27.3 %all-gather.5.cloned.1.call-done = f32[4,1,256,256]{3,2,1,0:T(8,128)} async-done(((f32[4,1,32,256]{3,2,1,0:T(8,128)}), f32[4,1,256,256]{3,2,1,0:T(8,128)}) %all-gather.5.cloned.1.call-update) | async-done | bytes 1048592 | tf_op jit(solution)/shard_map/all_gather | solution.py:53
  35.4 1.7 select_bitcast_fusion
  37.1 23.6 %all-gather.3.cloned.1.call-done = f32[4,1,256,256]{3,2,1,0:T(8,128)} async-done(((f32[4,1,32,256]{3,2,1,0:T(8,128)}), f32[4,1,256,256]{3,2,1,0:T(8,128)}) %all-gather.3.cloned.1.call-update) | async-done | bytes 1048592 | tf_op jit(solution)/shard_map/all_gather | solution.py:52
  60.7 1.7 select_bitcast_fusion.1
  64.2 11.9 %psum.37 = f32[256]{0:T(256)S(1)} all-reduce(f32[256]{0:T(256)S(1)} %bitcast.100), channel_id=1, replica_groups=mesh['row'=8,'col'=4] {'col'}, use_global_device_ids=true, to_apply=%region_2.3 | all-reduce | flops 256 | bytes 2048 | tf_op jit(solution)/shard_map/psum | solution.py:12
  76.1 25.7 %all-reduce.9.cloned.1.call-done = (f32[256,256]{1,0:T(8,128)}, f32[256,256]{1,0:T(8,128)}) async-done(((f32[256,256]{1,0:T(8,128)}, f32[256,256]{1,0:T(8,128)}), (f32[256,256]{1,0:T(8,128)}, f32[256,256]{1,0:T(8,128)})) %all-reduce.9.cloned.1.call-update) | async-done | bytes 524304 | tf_op jit(solution)/shard_map/psum | solution.py:12
  107.3 35.5 %all-reduce.5.cloned.1.call-done = f32[256,256]{0,1:T(8,128)} async-done(((f32[256,256]{0,1:T(8,128)}), f32[256,256]{0,1:T(8,128)}) %all-reduce.5.cloned.1.call-update) | async-done | bytes 262160 | tf_op jit(solution)/shard_map/psum | solution.py:12
  144.1 2.6 collective-permute-done
  148.5 23.7 %collective-permute-done.1 = f32[4,256,256]{1,2,0:T(8,128)S(1)} collective-permute-done((f32[4,256,256]{1,2,0:T(8,128)S(1)}, f32[4,256,256]{1,2,0:T(8,128)S(1)}, u32[]{:S(2)}, u32[]{:S(2)}) %collective-permute-start.1) | collective-permute-done | bytes 1048608 | tf_op jit(solution)/shard_map/ppermute | solution.py:99
  172.4 1.5 collective-permute-start.2
  174.0 2.3 dynamic-slice_bitcast_fusion
  178.5 29.7 %collective-permute-done.3 = bf16[256,1024]{1,0:T(8,128)(2,1)} collective-permute-done((bf16[256,1024]{1,0:T(8,128)(2,1)}, bf16[256,1024]{1,0:T(8,128)(2,1)}, u32[]{:S(2)}, u32[]{:S(2)}) %collective-permute-start.3) | collective-permute-done | bytes 524320 | tf_op jit(solution)/shard_map/ppermute | solution.py:18
  209.4 1.6 convolution_bitcast_fusion.1
  213.8 2.7 fusion.3
  220.9 35.6 %all-reduce.7.cloned.1.call-done = f32[256,256]{0,1:T(8,128)} async-done(((f32[256,256]{0,1:T(8,128)}), f32[256,256]{0,1:T(8,128)}) %all-reduce.7.cloned.1.call-update) | async-done | bytes 262160 | tf_op jit(solution)/shard_map/psum | solution.py:12
  257.7 2.6 collective-permute-done.5
  262.1 23.7 %collective-permute-done.6 = f32[4,256,256]{1,2,0:T(8,128)S(1)} collective-permute-done((f32[4,256,256]{1,2,0:T(8,128)S(1)}, f32[4,256,256]{1,2,0:T(8,128)S(1)}, u32[]{:S(2)}, u32[]{:S(2)}) %collective-permute-start.6) | collective-permute-done | bytes 1048608 | tf_op jit(solution)/shard_map/ppermute | solution.py:99
  286.0 1.5 collective-permute-start.7
  287.6 2.3 collective-permute-start.4
  289.9 10.5 %collective-permute-done.4 = bf16[256,1024]{1,0:T(8,128)(2,1)S(1)} collective-permute-done((bf16[256,1024]{1,0:T(8,128)(2,1)S(1)}, bf16[256,1024]{1,0:T(8,128)(2,1)S(1)}, u32[]{:S(2)}, u32[]{:S(2)}) %collective-permute-start.4) | collective-permute-done | bytes 524320 | tf_op jit(solution)/shard_map/ppermute | solution.py:18
  302.0 19.8 %collective-permute-done.8 = bf16[256,1024]{1,0:T(8,128)(2,1)} collective-permute-done((bf16[256,1024]{1,0:T(8,128)(2,1)}, bf16[256,1024]{1,0:T(8,128)(2,1)}, u32[]{:S(2)}, u32[]{:S(2)}) %collective-permute-start.8) | collective-permute-done | bytes 524320 | tf_op jit(solution)/shard_map/ppermute | solution.py:18
  323.0 1.6 convolution_bitcast_fusion
  327.3 3.2 fusion.1
  330.5 3.6 %copy.32 = f32[256,1,1024]{2,1,0:T(1,128)} copy(f32[256,1,1024]{0,2,1:T(8,128)} %bitcast.92) | data formatting | bytes 2097152 | tf_op jit(solution)/shard_map/reshape | solution.py:120
  (82 shorter events, 30.9 us)
Async XLA Ops:
  6.5 55.9 %copy-start.8 = (f32[256,1,1024]{2,1,0:T(1,128)S(1)}, f32[256,1,1024]{2,1,0:T(1,128)}, u32[]{:S(2)}) copy-start(f32[256,1,1024]{2,1,0:T(1,128)} %param.6) | copy-start | bytes 3145732
  6.5 28.8 %all-gather.5.cloned.1.call-start = ((), (), s32[]{:S(2)}) async-start(), calls=%async_computation.1 | async-start | bytes 1179648 | tf_op jit(solution)/shard_map/all_gather | solution.py:53
  7.3 53.4 %all-gather.3.cloned.1.call-start = ((), (), s32[]{:S(2)}) async-start(), calls=%async_computation | async-start | bytes 1179648 | tf_op jit(solution)/shard_map/all_gather | solution.py:52
  8.0 93.8 %all-reduce.9.cloned.1.call-start = ((), (), s32[]{:S(2)}) async-start(), calls=%async_computation.4 | async-start | bytes 1048576 | tf_op jit(solution)/shard_map/psum | solution.py:12
  62.4 80.5 %all-reduce.5.cloned.1.call-start = ((), (), s32[]{:S(2)}) async-start(), calls=%async_computation.2 | async-start | bytes 524288 | tf_op jit(solution)/shard_map/psum | solution.py:12
  103.2 1.4 copy-start.7
  106.4 37.6 %copy-start.5 = (f32[4,256,256]{1,2,0:T(8,128)}, f32[4,256,256]{1,2,0:T(8,128)S(1)}, u32[]{:S(2)}) copy-start(f32[4,256,256]{1,2,0:T(8,128)S(1)} %get-tuple-element.12) | copy-start | bytes 3145732
  107.2 149.2 %all-reduce.7.cloned.1.call-start = ((), (), s32[]{:S(2)}) async-start(), calls=%async_computation.3 | async-start | bytes 524288 | tf_op jit(solution)/shard_map/psum | solution.py:12
  142.8 3.9 %copy-start = (f32[256,256]{0,1:T(8,128)S(1)}, f32[256,256]{0,1:T(8,128)}, u32[]{:S(2)}) copy-start(f32[256,256]{0,1:T(8,128)} %all-reduce.5.cloned.1.call-done) | copy-start | bytes 786436
  144.0 2.7 collective-permute-start
  146.9 25.3 %collective-permute-start.1 = (f32[4,256,256]{1,2,0:T(8,128)S(1)}, f32[4,256,256]{1,2,0:T(8,128)S(1)}, u32[]{:S(2)}, u32[]{:S(2)}) collective-permute-start(f32[4,256,256]{1,2,0:T(8,128)S(1)} %fusion.30), channel_id=1, source_target_pairs={{0,8},{4,12},{8,0},{12,4},{16,24},{20,28},{24,16},{28,20},{1,9},{5... | collective-permute-start | bytes 3145736 | tf_op jit(solution)/shard_map/ppermute | solution.py:99
  172.4 3.9 %copy-start.2 = (f32[4,256,256]{1,2,0:T(8,128)}, f32[4,256,256]{1,2,0:T(8,128)S(1)}, u32[]{:S(2)}) copy-start(f32[4,256,256]{1,2,0:T(8,128)S(1)} %fusion.60) | copy-start | bytes 3145732
  172.4 38.6 %collective-permute-start.2 = (f32[4,256,256]{1,2,0:T(8,128)S(1)}, f32[4,256,256]{1,2,0:T(8,128)}, u32[]{:S(2)}, u32[]{:S(2)}) collective-permute-start(f32[4,256,256]{1,2,0:T(8,128)S(1)} %fusion.60), channel_id=1, source_target_pairs={{0,16},{4,20},{8,24},{12,28},{16,0},{20,4},{24,8},{28,12},{1,17},{... | collective-permute-start | bytes 3145736 | tf_op jit(solution)/shard_map/ppermute | solution.py:99
  174.0 2.9 copy-start.10
  176.3 31.9 %collective-permute-start.3 = (bf16[256,1024]{1,0:T(8,128)(2,1)}, bf16[256,1024]{1,0:T(8,128)(2,1)}, u32[]{:S(2)}, u32[]{:S(2)}) collective-permute-start(bf16[256,1024]{1,0:T(8,128)(2,1)} %get-tuple-element.8), channel_id=1, source_target_pairs={{16,0},{20,4},{24,8},{28,12},{0,16},{4,20},{8,24},{12,28},{17,1},{... | collective-permute-start | bytes 1572872 | tf_op jit(solution)/shard_map/ppermute | solution.py:18
  209.4 1.7 copy-start.3
  213.8 2.7 copy-start.9
  256.5 3.9 %copy-start.1 = (f32[256,256]{0,1:T(8,128)S(1)}, f32[256,256]{0,1:T(8,128)}, u32[]{:S(2)}) copy-start(f32[256,256]{0,1:T(8,128)} %all-reduce.7.cloned.1.call-done) | copy-start | bytes 786436
  257.6 2.7 collective-permute-start.5
  260.5 27.0 %copy-start.11 = (bf16[256,1,1024]{2,0,1:T(8,128)(2,1)S(1)}, bf16[256,1,1024]{2,0,1:T(8,128)(2,1)}, u32[]{:S(2)}) copy-start(bf16[256,1,1024]{2,0,1:T(8,128)(2,1)} %param.7) | copy-start | bytes 1572868
  260.5 25.3 %collective-permute-start.6 = (f32[4,256,256]{1,2,0:T(8,128)S(1)}, f32[4,256,256]{1,2,0:T(8,128)S(1)}, u32[]{:S(2)}, u32[]{:S(2)}) collective-permute-start(f32[4,256,256]{1,2,0:T(8,128)S(1)} %fusion.31), channel_id=1, source_target_pairs={{0,8},{4,12},{8,0},{12,4},{16,24},{20,28},{24,16},{28,20},{1,9},{5... | collective-permute-start | bytes 3145736 | tf_op jit(solution)/shard_map/ppermute | solution.py:99
  286.0 38.6 %collective-permute-start.7 = (f32[4,256,256]{1,2,0:T(8,128)S(1)}, f32[4,256,256]{1,2,0:T(8,128)}, u32[]{:S(2)}, u32[]{:S(2)}) collective-permute-start(f32[4,256,256]{1,2,0:T(8,128)S(1)} %fusion.59), channel_id=1, source_target_pairs={{0,16},{4,20},{8,24},{12,28},{16,0},{20,4},{24,8},{28,12},{1,17},{... | collective-permute-start | bytes 3145736 | tf_op jit(solution)/shard_map/ppermute | solution.py:99
  287.6 12.8 %collective-permute-start.4 = (bf16[256,1024]{1,0:T(8,128)(2,1)S(1)}, bf16[256,1024]{1,0:T(8,128)(2,1)S(1)}, u32[]{:S(2)}, u32[]{:S(2)}) collective-permute-start(bf16[256,1024]{1,0:T(8,128)(2,1)S(1)} %bitcast.99), channel_id=1, source_target_pairs={{1,0},{2,1},{3,2},{0,3},{5,4},{6,5},{7,6},{4,7},{9,8},{10,9},{11,1... | collective-permute-start | bytes 1572872 | tf_op jit(solution)/shard_map/ppermute | solution.py:18
  289.9 31.9 %collective-permute-start.8 = (bf16[256,1024]{1,0:T(8,128)(2,1)}, bf16[256,1024]{1,0:T(8,128)(2,1)}, u32[]{:S(2)}, u32[]{:S(2)}) collective-permute-start(bf16[256,1024]{1,0:T(8,128)(2,1)} %get-tuple-element.7), channel_id=1, source_target_pairs={{20,0},{24,4},{28,8},{0,12},{4,16},{8,20},{12,24},{16,28},{21,1},{... | collective-permute-start | bytes 1572872 | tf_op jit(solution)/shard_map/ppermute | solution.py:18
  (3 other events, 2.8 us)
Sparse Core Ops, SparseCore 0:
  9.2 26.0 all-gather.4
  37.3 23.3 all-gather.2
  63.1 38.7 all-reduce.8
  107.4 35.4 all-reduce.4
  221.0 35.4 all-reduce.6
